TPU v7x, 32 devices: a whole 2x2x4 slice. The times are simulated.
32 devices in a mesh: section: 2 (over y), mp: 16 (over z, x, core).
Axes of the slice: x: 2, y: 2, z: 4, core: 2. Of those that a mesh axis runs over, the one named last changes fastest.
Arguments:
- features: bfloat16 [4, 32, 8192], P(None, None, 'mp'), may hold values from -6 to 6
- labels: int32 [4, 32], replicated, may hold values 0 or 1
- weights: bfloat16 [2, 8192, 8192], P('section', None, 'mp'), may hold values from -1.78986404 to 1.78986404
- vectors: float32 [2, 8192], P('section', 'mp'), may hold values from -6 to 6
- head_weight: float32 [8192], P('mp'), may hold values from -0.0625 to 0.0625
Outputs:
- weight_grad: bfloat16 [2, 8192, 8192], P('section', None, 'mp')
- new_vectors: float32 [2, 8192], P('section', 'mp')
- rank_coef: float32 [2], P('section')
All inputs are finite; a program needn't handle non-finite values.
Results may differ from a plain program's by a relative error of at most 0.015.
Values may be sent and summed in bfloat16 or wider, within the bound.
No kernel may reach another device: no remote copies, remote signals or barrier semaphores. Data moves between devices by JAX's collectives and lax.ppermute only.
A program may use at most 64 MiB of HBM per device.

v0:
```python
import jax
import jax.numpy as jnp
from jax import lax
from jax.sharding import PartitionSpec as P

loss_scale = 32.0
tiny_eps = 1e-06


def shifted(block, axis, distance):
    devices = range(lax.axis_size(axis))
    route = [(i - distance, i) for i in devices if i - distance in devices]
    return lax.ppermute(block, axis, route)


def silu_slope(pre_act):
    gate_val = jax.nn.sigmoid(pre_act)
    return gate_val * (1.0 + pre_act * (1.0 - gate_val))


def keep_slot(stored, update, micro_slot, is_live):
    previous = lax.dynamic_index_in_dim(stored, micro_slot, 0, keepdims=False)
    return lax.dynamic_update_index_in_dim(
        stored, jnp.where(is_live, update, previous), micro_slot, 0
    )


def power_step(weight, vector_u):
    vector_bf = vector_u.astype(jnp.bfloat16)
    left_sum = lax.psum(jnp.dot(weight, vector_bf, preferred_element_type=jnp.float32), "mp")
    vector_v = (left_sum * lax.rsqrt(jnp.sum(left_sum * left_sum) + tiny_eps)).astype(jnp.bfloat16)
    right_part = jnp.dot(vector_v, weight, preferred_element_type=jnp.float32)
    norm_total = lax.psum(jnp.sum(right_part * right_part), "mp")
    spectral = jnp.sqrt(norm_total + tiny_eps)
    return (spectral, right_part / spectral)


def on_device(features, labels, weights, vectors, head_weight):
    weight = weights[0]
    vector_u = vectors[0]
    micro_count, batch_rows, local_cols = features.shape
    full_width = weight.shape[0]
    sections = lax.axis_size("section")
    section_index = lax.axis_index("section")
    tick_count = micro_count + sections - 1
    sign_all = (2 * labels - 1).astype(jnp.float32)
    spectral_init, new_init = power_step(weight, vector_u)

    def forward_tick(tick_now, state_all):
        incoming, inputs_all, pre_all, logits_all, spectral, new_u = state_all
        micro_index = tick_now - section_index
        is_live = (micro_index >= 0) & (micro_index < micro_count)
        micro_slot = jnp.clip(micro_index, 0, micro_count - 1)
        first_input = lax.dynamic_index_in_dim(features, micro_slot, 0, keepdims=False)
        layer_in = jnp.where(section_index == 0, first_input, incoming)
        shard_piece = lax.all_gather(layer_in, "mp", axis=1, tiled=True)
        accum_part = jnp.dot(shard_piece, weight, preferred_element_type=jnp.float32)
        whole_rows = shard_piece
        accum_part, whole_rows = (accum_part, whole_rows)
        pre_act = accum_part / spectral
        layer_out = (layer_in.astype(jnp.float32) + jax.nn.silu(pre_act)).astype(jnp.bfloat16)
        partial_logit = jnp.sum(layer_out.astype(jnp.float32) * head_weight[None, :], axis=1)
        inputs_all = keep_slot(inputs_all, whole_rows, micro_slot, is_live)
        pre_all = keep_slot(pre_all, pre_act, micro_slot, is_live)
        logits_all = keep_slot(
            logits_all, partial_logit, micro_slot, is_live & (section_index == sections - 1)
        )
        incoming = shifted(layer_out, "section", 1)
        return (incoming, inputs_all, pre_all, logits_all, spectral, new_u)

    start_state = (
        jnp.zeros((batch_rows, local_cols), jnp.bfloat16),
        jnp.zeros((micro_count, batch_rows, full_width), jnp.bfloat16),
        jnp.zeros((micro_count, batch_rows, local_cols), jnp.float32),
        jnp.zeros((micro_count, batch_rows), jnp.float32),
        spectral_init,
        new_init,
    )
    _, inputs_all, pre_all, partial_logits, spectral, new_u = lax.fori_loop(
        0, tick_count, forward_tick, start_state
    )
    logits_all = lax.psum(partial_logits, "mp")

    def backward_tick(tick_now, state_all):
        incoming, grad_all = state_all
        micro_index = tick_now - (sections - 1 - section_index)
        is_live = (micro_index >= 0) & (micro_index < micro_count)
        micro_slot = jnp.clip(micro_index, 0, micro_count - 1)
        sign_row = lax.dynamic_index_in_dim(sign_all, micro_slot, 0, keepdims=False)
        logit_row = lax.dynamic_index_in_dim(logits_all, micro_slot, 0, keepdims=False)
        top_scale = -loss_scale * sign_row * jax.nn.sigmoid(-sign_row * logit_row)
        top_grad = (top_scale[:, None] * head_weight[None, :]).astype(jnp.bfloat16)
        grad_out = jnp.where(section_index == sections - 1, top_grad, incoming)
        pre_act = lax.dynamic_index_in_dim(pre_all, micro_slot, 0, keepdims=False)
        grad_pre = (grad_out.astype(jnp.float32) * silu_slope(pre_act)).astype(jnp.bfloat16)
        partial_term = lax.dot_general(
            grad_pre, weight, (((1,), (1,)), ((), ())), preferred_element_type=jnp.float32
        )
        received = lax.all_to_all(
            partial_term.astype(jnp.bfloat16), "mp", split_axis=1, concat_axis=0, tiled=True
        ).astype(partial_term.dtype)
        back_sum = jnp.sum(received.reshape(-1, batch_rows, local_cols), axis=0)
        grad_in = (grad_out.astype(jnp.float32) + back_sum / spectral).astype(jnp.bfloat16)
        grad_all = keep_slot(grad_all, grad_pre, micro_slot, is_live)
        incoming = shifted(grad_in, "section", -1)
        return (incoming, grad_all)

    back_state = (
        jnp.zeros((batch_rows, local_cols), jnp.bfloat16),
        jnp.zeros((micro_count, batch_rows, local_cols), jnp.bfloat16),
    )
    _, grad_all = lax.fori_loop(0, tick_count, backward_tick, back_state)
    whole_rows = inputs_all.reshape(micro_count * batch_rows, full_width)
    grad_rows = grad_all.reshape(micro_count * batch_rows, local_cols)
    outer_sum = lax.dot_general(
        whole_rows, grad_rows, (((0,), (0,)), ((), ())), preferred_element_type=jnp.float32
    )
    weight_grad = (outer_sum / spectral).astype(jnp.bfloat16)
    inner_total = lax.psum(jnp.sum(outer_sum * weight.astype(jnp.float32)), "mp")
    rank_coef = inner_total / (spectral * spectral)
    return (weight_grad[None], new_u[None], rank_coef.reshape(1))


def solution(mesh):
    placed = (P(None, None, "mp"), P(), P("section", None, "mp"), P("section", "mp"), P("mp"))
    return jax.shard_map(
        on_device,
        mesh=mesh,
        in_specs=placed,
        out_specs=(P("section", None, "mp"), P("section", "mp"), P("section")),
        check_vma=False,
    )
```

profile of v0, /device:TPU:0, one launch (start us, length us, event | category | flops | bytes accessed | tf_op | source)
XLA Modules:
  0.0 495.4 jit_solution(9324954132209440340)
XLA Ops:
  6.3 63.0 %psum.28 = f32[8192]{0:T(1024)S(1)} all-reduce(f32[8192]{0:T(1024)S(1)} %bitcast.113), channel_id=1, replica_groups=mesh['section'=2,'mp'=16] {'mp'}, use_global_device_ids=true, to_apply=%region_0.0 | all-reduce | flops 8192 | bytes 65536 | tf_op jit(solution)/shard_map/psum | solution.py:30
  75.8 30.1 %psum.29 = f32[]{:T(128)} all-reduce(f32[]{:T(128)} %multiply_reduce_fusion.2), channel_id=1, replica_groups=mesh['section'=2,'mp'=16] {'mp'}, use_global_device_ids=true, to_apply=%region_3.0 | all-reduce | flops 1 | bytes 8 | tf_op jit(solution)/shard_map/psum | solution.py:33
  107.4 158.8 %while.37 = (s32[]{:T(128)}, bf16[32,512]{1,0:T(8,128)(2,1)}, bf16[4,32,8192]{2,1,0:T(8,128)(2,1)S(1)}, f32[4,32,512]{2,1,0:T(8,128)S(1)}, f32[4,32]{1,0:T(4,128...) while((s32[]{:T(128)}, bf16[32,512]{1,0:T(8,128)(2,1)}, ...), condition=%wide.region_6.7_spmd, body=%wide.region_4.6_spmd.sunk | while | flops 268910592 | bytes 12782621 | solution.py:79
  108.2 18.7 %all_gather.9 = bf16[32,8192]{1,0:T(8,128)(2,1)S(1)} all-gather(bf16[32,512]{1,0:T(8,128)(2,1)S(1)} %bitcast_select_fusion.5), channel_id=1, replica_groups=mesh['section'=2,'mp'=16] {'mp'}, dimensions={1}, use_global_device_ids=true | all-gather | bytes 557056 | tf_op jit(solution)/shard_map/while/body/eval_jaxpr/all_gather | solution.py:56
  126.9 5.7 %multiply_reduce_fusion.4 = (f32[32]{0:T(128)S(1)}, bf16[32,512]{1,0:T(8,128)(2,1)}, f32[32,512]{1,0:T(8,128)S(1)}) fusion(f32[512]{0:T(512)S(1)} %get-tuple-element.704, bf16[32,512]{1,0:T(8,128)(2,1)S(1)} %bitcast_select_fusion.5, f32[]{:T(128)} %get-tuple-element.702, bf16[32,8192]{1,0:T(8,128)(2,1)S(1)} %all_gather.9, ...), kind=kOutput, calls=%fused_computation.5.clone.1 | convolution fusion | flops 268615648 | bytes 9046148 | tf_op jit(solution)/shard_map/while/body/eval_jaxpr/dot_general | solution.py:57
  138.6 20.4 %all_gather.9 = bf16[32,8192]{1,0:T(8,128)(2,1)S(1)} all-gather(bf16[32,512]{1,0:T(8,128)(2,1)S(1)} %bitcast_select_fusion.5), channel_id=1, replica_groups=mesh['section'=2,'mp'=16] {'mp'}, dimensions={1}, use_global_device_ids=true | all-gather | bytes 557056 | tf_op jit(solution)/shard_map/while/body/eval_jaxpr/all_gather | solution.py:56
  171.6 18.7 %all_gather.9 = bf16[32,8192]{1,0:T(8,128)(2,1)S(1)} all-gather(bf16[32,512]{1,0:T(8,128)(2,1)S(1)} %bitcast_select_fusion.5), channel_id=1, replica_groups=mesh['section'=2,'mp'=16] {'mp'}, dimensions={1}, use_global_device_ids=true | all-gather | bytes 557056 | tf_op jit(solution)/shard_map/while/body/eval_jaxpr/all_gather | solution.py:56
  190.3 5.7 %multiply_reduce_fusion.4 = (f32[32]{0:T(128)S(1)}, bf16[32,512]{1,0:T(8,128)(2,1)}, f32[32,512]{1,0:T(8,128)S(1)}) fusion(f32[512]{0:T(512)S(1)} %get-tuple-element.704, bf16[32,512]{1,0:T(8,128)(2,1)S(1)} %bitcast_select_fusion.5, f32[]{:T(128)} %get-tuple-element.702, bf16[32,8192]{1,0:T(8,128)(2,1)S(1)} %all_gather.9, ...), kind=kOutput, calls=%fused_computation.5.clone.1 | convolution fusion | flops 268615648 | bytes 9046148 | tf_op jit(solution)/shard_map/while/body/eval_jaxpr/dot_general | solution.py:57
  202.8 20.4 %all_gather.9 = bf16[32,8192]{1,0:T(8,128)(2,1)S(1)} all-gather(bf16[32,512]{1,0:T(8,128)(2,1)S(1)} %bitcast_select_fusion.5), channel_id=1, replica_groups=mesh['section'=2,'mp'=16] {'mp'}, dimensions={1}, use_global_device_ids=true | all-gather | bytes 557056 | tf_op jit(solution)/shard_map/while/body/eval_jaxpr/all_gather | solution.py:56
  235.8 18.7 %all_gather.9 = bf16[32,8192]{1,0:T(8,128)(2,1)S(1)} all-gather(bf16[32,512]{1,0:T(8,128)(2,1)S(1)} %bitcast_select_fusion.5), channel_id=1, replica_groups=mesh['section'=2,'mp'=16] {'mp'}, dimensions={1}, use_global_device_ids=true | all-gather | bytes 557056 | tf_op jit(solution)/shard_map/while/body/eval_jaxpr/all_gather | solution.py:56
  266.2 30.4 %psum.30 = f32[4,32]{1,0:T(4,128)S(1)} all-reduce(f32[4,32]{1,0:T(4,128)S(1)} %get-tuple-element.461), channel_id=1, replica_groups=mesh['section'=2,'mp'=16] {'mp'}, use_global_device_ids=true, to_apply=%region_7.8 | all-reduce | flops 128 | bytes 1024 | tf_op jit(solution)/shard_map/psum | solution.py:82
  297.4 155.4 %while.38 = (s32[]{:T(128)}, bf16[32,512]{1,0:T(8,128)(2,1)S(1)}, bf16[4,32,512]{2,1,0:T(8,128)(2,1)S(1)}, pred[]{:T(512)}, s32[]{:T(128)}, /*index=5*/f32[4,32]...) while((s32[]{:T(128)}, bf16[32,512]{1,0:T(8,128)(2,1)S(1)}, ...), condition=%wide.region_10.11_spmd, body=%wide.region_8.10_spmd.sunk | while | flops 269762784 | bytes 12787494 | solution.py:112
  297.4 5.9 %convolution_convert_fusion.2 = bf16[32,8192]{1,0:T(8,128)(2,1)S(1)} fusion(bf16[8192,512]{1,0:T(8,128)(2,1)} %get-tuple-element.748, f32[4,32,512]{2,1,0:T(8,128)S(1)} %get-tuple-element.747, s32[]{:T(128)S(6)} %min.21, bf16[32,512]{1,0:T(8,128)(2,1)S(1)} %get-tuple-element.725, f32[512]{0:T(512)S(1)} %get-tuple-element.746, f32[32]{0:T(128)S(1)} %fusion.37, ...), kind=kOutput, calls=%fused_computation.12.clone.1 | convolution fusion | flops 268910592 | bytes 9013765 | tf_op jit(solution)/shard_map/while/body/eval_jaxpr/dot_general | solution.py:96
  307.8 14.2 %all-to-all-done = bf16[32,16,512]{2,0,1:T(8,128)(2,1)S(1)} async-done(((bf16[32,16,512]{2,0,1:T(8,128)(2,1)}), bf16[32,16,512]{2,0,1:T(8,128)(2,1)S(1)}, u32[]{:S(2)}, u32[]{:S(2)}) %all-to-all-start) | async-done | bytes 524320 | tf_op jit(solution)/shard_map/while/body/eval_jaxpr/all_to_all | solution.py:99
  328.0 5.9 %convolution_convert_fusion.2 = bf16[32,8192]{1,0:T(8,128)(2,1)S(1)} fusion(bf16[8192,512]{1,0:T(8,128)(2,1)} %get-tuple-element.748, f32[4,32,512]{2,1,0:T(8,128)S(1)} %get-tuple-element.747, s32[]{:T(128)S(6)} %min.21, bf16[32,512]{1,0:T(8,128)(2,1)S(1)} %get-tuple-element.725, f32[512]{0:T(512)S(1)} %get-tuple-element.746, f32[32]{0:T(128)S(1)} %fusion.37, ...), kind=kOutput, calls=%fused_computation.12.clone.1 | convolution fusion | flops 268910592 | bytes 9013765 | tf_op jit(solution)/shard_map/while/body/eval_jaxpr/dot_general | solution.py:96
  338.9 14.2 %all-to-all-done = bf16[32,16,512]{2,0,1:T(8,128)(2,1)S(1)} async-done(((bf16[32,16,512]{2,0,1:T(8,128)(2,1)}), bf16[32,16,512]{2,0,1:T(8,128)(2,1)S(1)}, u32[]{:S(2)}, u32[]{:S(2)}) %all-to-all-start) | async-done | bytes 524320 | tf_op jit(solution)/shard_map/while/body/eval_jaxpr/all_to_all | solution.py:99
  359.1 5.9 %convolution_convert_fusion.2 = bf16[32,8192]{1,0:T(8,128)(2,1)S(1)} fusion(bf16[8192,512]{1,0:T(8,128)(2,1)} %get-tuple-element.748, f32[4,32,512]{2,1,0:T(8,128)S(1)} %get-tuple-element.747, s32[]{:T(128)S(6)} %min.21, bf16[32,512]{1,0:T(8,128)(2,1)S(1)} %get-tuple-element.725, f32[512]{0:T(512)S(1)} %get-tuple-element.746, f32[32]{0:T(128)S(1)} %fusion.37, ...), kind=kOutput, calls=%fused_computation.12.clone.1 | convolution fusion | flops 268910592 | bytes 9013765 | tf_op jit(solution)/shard_map/while/body/eval_jaxpr/dot_general | solution.py:96
  370.1 14.2 %all-to-all-done = bf16[32,16,512]{2,0,1:T(8,128)(2,1)S(1)} async-done(((bf16[32,16,512]{2,0,1:T(8,128)(2,1)}), bf16[32,16,512]{2,0,1:T(8,128)(2,1)S(1)}, u32[]{:S(2)}, u32[]{:S(2)}) %all-to-all-start) | async-done | bytes 524320 | tf_op jit(solution)/shard_map/while/body/eval_jaxpr/all_to_all | solution.py:99
  390.4 5.9 %convolution_convert_fusion.2 = bf16[32,8192]{1,0:T(8,128)(2,1)S(1)} fusion(bf16[8192,512]{1,0:T(8,128)(2,1)} %get-tuple-element.748, f32[4,32,512]{2,1,0:T(8,128)S(1)} %get-tuple-element.747, s32[]{:T(128)S(6)} %min.21, bf16[32,512]{1,0:T(8,128)(2,1)S(1)} %get-tuple-element.725, f32[512]{0:T(512)S(1)} %get-tuple-element.746, f32[32]{0:T(128)S(1)} %fusion.37, ...), kind=kOutput, calls=%fused_computation.12.clone.1 | convolution fusion | flops 268910592 | bytes 9013765 | tf_op jit(solution)/shard_map/while/body/eval_jaxpr/dot_general | solution.py:96
  401.3 14.2 %all-to-all-done = bf16[32,16,512]{2,0,1:T(8,128)(2,1)S(1)} async-done(((bf16[32,16,512]{2,0,1:T(8,128)(2,1)}), bf16[32,16,512]{2,0,1:T(8,128)(2,1)S(1)}, u32[]{:S(2)}, u32[]{:S(2)}) %all-to-all-start) | async-done | bytes 524320 | tf_op jit(solution)/shard_map/while/body/eval_jaxpr/all_to_all | solution.py:99
  421.6 5.9 %convolution_convert_fusion.2 = bf16[32,8192]{1,0:T(8,128)(2,1)S(1)} fusion(bf16[8192,512]{1,0:T(8,128)(2,1)} %get-tuple-element.748, f32[4,32,512]{2,1,0:T(8,128)S(1)} %get-tuple-element.747, s32[]{:T(128)S(6)} %min.21, bf16[32,512]{1,0:T(8,128)(2,1)S(1)} %get-tuple-element.725, f32[512]{0:T(512)S(1)} %get-tuple-element.746, f32[32]{0:T(128)S(1)} %fusion.37, ...), kind=kOutput, calls=%fused_computation.12.clone.1 | convolution fusion | flops 268910592 | bytes 9013765 | tf_op jit(solution)/shard_map/while/body/eval_jaxpr/dot_general | solution.py:96
  432.6 14.2 %all-to-all-done = bf16[32,16,512]{2,0,1:T(8,128)(2,1)S(1)} async-done(((bf16[32,16,512]{2,0,1:T(8,128)(2,1)}), bf16[32,16,512]{2,0,1:T(8,128)(2,1)S(1)}, u32[]{:S(2)}, u32[]{:S(2)}) %all-to-all-start) | async-done | bytes 524320 | tf_op jit(solution)/shard_map/while/body/eval_jaxpr/all_to_all | solution.py:99
  452.8 8.5 %fusion.13 = (f32[]{:T(128)}, bf16[1,8192,512]{2,1,0:T(8,128)(2,1)}) fusion(bf16[1,8192,512]{2,1,0:T(8,128)(2,1)} %bitcast.111, f32[]{:T(128)} %sqrt.3, bf16[4,32,8192]{2,1,0:T(8,128)(2,1)S(1)} %get-tuple-element.460, bf16[4,32,512]{2,1,0:T(8,128)(2,1)S(1)} %get-tuple-element.463), kind=kOutput, calls=%fused_computation.40 | convolution fusion | flops 1094713344 | bytes 19005448 | tf_op jit(solution)/shard_map/dot_general | solution.py:115
  461.3 31.7 %psum.31 = f32[]{:T(128)} all-reduce(f32[]{:T(128)} %get-tuple-element.513), channel_id=1, replica_groups=mesh['section'=2,'mp'=16] {'mp'}, use_global_device_ids=true, to_apply=%region_12.13 | all-reduce | flops 1 | bytes 8 | tf_op jit(solution)/shard_map/psum | solution.py:119
  (114 shorter events, 118.2 us)
Async XLA Ops:
  70.6 36.8 %copy-start = (f32[512]{0:T(512)S(1)}, f32[512]{0:T(512)}, u32[]{:S(2)}) copy-start(f32[512]{0:T(512)} %param.13) | copy-start | bytes 6148
  132.5 5.3 %collective-permute-start = (bf16[32,512]{1,0:T(8,128)(2,1)}, bf16[32,512]{1,0:T(8,128)(2,1)}, u32[]{:S(2)}, u32[]{:S(2)}) collective-permute-start(bf16[32,512]{1,0:T(8,128)(2,1)} %get-tuple-element.647), channel_id=1, source_target_pairs={{0,16},{1,17},{2,18},{3,19},{4,20},{5,21},{6,22},{7,23},{8,24},{9,... | collective-permute-start | bytes 98312 | tf_op jit(solution)/shard_map/while/body/eval_jaxpr/ppermute | solution.py:13
  164.7 6.1 %collective-permute-start = (bf16[32,512]{1,0:T(8,128)(2,1)}, bf16[32,512]{1,0:T(8,128)(2,1)}, u32[]{:S(2)}, u32[]{:S(2)}) collective-permute-start(bf16[32,512]{1,0:T(8,128)(2,1)} %get-tuple-element.647), channel_id=1, source_target_pairs={{0,16},{1,17},{2,18},{3,19},{4,20},{5,21},{6,22},{7,23},{8,24},{9,... | collective-permute-start | bytes 98312 | tf_op jit(solution)/shard_map/while/body/eval_jaxpr/ppermute | solution.py:13
  195.9 6.1 %collective-permute-start = (bf16[32,512]{1,0:T(8,128)(2,1)}, bf16[32,512]{1,0:T(8,128)(2,1)}, u32[]{:S(2)}, u32[]{:S(2)}) collective-permute-start(bf16[32,512]{1,0:T(8,128)(2,1)} %get-tuple-element.647), channel_id=1, source_target_pairs={{0,16},{1,17},{2,18},{3,19},{4,20},{5,21},{6,22},{7,23},{8,24},{9,... | collective-permute-start | bytes 98312 | tf_op jit(solution)/shard_map/while/body/eval_jaxpr/ppermute | solution.py:13
  228.9 6.1 %collective-permute-start = (bf16[32,512]{1,0:T(8,128)(2,1)}, bf16[32,512]{1,0:T(8,128)(2,1)}, u32[]{:S(2)}, u32[]{:S(2)}) collective-permute-start(bf16[32,512]{1,0:T(8,128)(2,1)} %get-tuple-element.647), channel_id=1, source_target_pairs={{0,16},{1,17},{2,18},{3,19},{4,20},{5,21},{6,22},{7,23},{8,24},{9,... | collective-permute-start | bytes 98312 | tf_op jit(solution)/shard_map/while/body/eval_jaxpr/ppermute | solution.py:13
  260.1 6.1 %collective-permute-start = (bf16[32,512]{1,0:T(8,128)(2,1)}, bf16[32,512]{1,0:T(8,128)(2,1)}, u32[]{:S(2)}, u32[]{:S(2)}) collective-permute-start(bf16[32,512]{1,0:T(8,128)(2,1)} %get-tuple-element.647), channel_id=1, source_target_pairs={{0,16},{1,17},{2,18},{3,19},{4,20},{5,21},{6,22},{7,23},{8,24},{9,... | collective-permute-start | bytes 98312 | tf_op jit(solution)/shard_map/while/body/eval_jaxpr/ppermute | solution.py:13
  304.2 17.8 %all-to-all-start = ((bf16[32,16,512]{2,0,1:T(8,128)(2,1)}), bf16[32,16,512]{2,0,1:T(8,128)(2,1)S(1)}, u32[]{:S(2)}, u32[]{:S(2)}) async-start(bf16[32,16,512]{2,0,1:T(8,128)(2,1)} %bitcast.109), calls=%async_computation | async-start | bytes 1048576 | tf_op jit(solution)/shard_map/while/body/eval_jaxpr/all_to_all | solution.py:99
  322.2 5.8 %collective-permute-start.1 = (bf16[32,512]{1,0:T(8,128)(2,1)S(1)}, bf16[32,512]{1,0:T(8,128)(2,1)S(1)}, u32[]{:S(2)}, u32[]{:S(2)}) collective-permute-start(bf16[32,512]{1,0:T(8,128)(2,1)S(1)} %fusion.38), channel_id=1, source_target_pairs={{16,0},{17,1},{18,2},{19,3},{20,4},{21,5},{22,6},{23,7},{24,8},{25... | collective-permute-start | bytes 98312 | tf_op jit(solution)/shard_map/while/body/eval_jaxpr/ppermute | solution.py:13
  334.8 18.4 %all-to-all-start = ((bf16[32,16,512]{2,0,1:T(8,128)(2,1)}), bf16[32,16,512]{2,0,1:T(8,128)(2,1)S(1)}, u32[]{:S(2)}, u32[]{:S(2)}) async-start(bf16[32,16,512]{2,0,1:T(8,128)(2,1)} %bitcast.109), calls=%async_computation | async-start | bytes 1048576 | tf_op jit(solution)/shard_map/while/body/eval_jaxpr/all_to_all | solution.py:99
  353.3 5.8 %collective-permute-start.1 = (bf16[32,512]{1,0:T(8,128)(2,1)S(1)}, bf16[32,512]{1,0:T(8,128)(2,1)S(1)}, u32[]{:S(2)}, u32[]{:S(2)}) collective-permute-start(bf16[32,512]{1,0:T(8,128)(2,1)S(1)} %fusion.38), channel_id=1, source_target_pairs={{16,0},{17,1},{18,2},{19,3},{20,4},{21,5},{22,6},{23,7},{24,8},{25... | collective-permute-start | bytes 98312 | tf_op jit(solution)/shard_map/while/body/eval_jaxpr/ppermute | solution.py:13
  365.9 18.4 %all-to-all-start = ((bf16[32,16,512]{2,0,1:T(8,128)(2,1)}), bf16[32,16,512]{2,0,1:T(8,128)(2,1)S(1)}, u32[]{:S(2)}, u32[]{:S(2)}) async-start(bf16[32,16,512]{2,0,1:T(8,128)(2,1)} %bitcast.109), calls=%async_computation | async-start | bytes 1048576 | tf_op jit(solution)/shard_map/while/body/eval_jaxpr/all_to_all | solution.py:99
  384.5 5.8 %collective-permute-start.1 = (bf16[32,512]{1,0:T(8,128)(2,1)S(1)}, bf16[32,512]{1,0:T(8,128)(2,1)S(1)}, u32[]{:S(2)}, u32[]{:S(2)}) collective-permute-start(bf16[32,512]{1,0:T(8,128)(2,1)S(1)} %fusion.38), channel_id=1, source_target_pairs={{16,0},{17,1},{18,2},{19,3},{20,4},{21,5},{22,6},{23,7},{24,8},{25... | collective-permute-start | bytes 98312 | tf_op jit(solution)/shard_map/while/body/eval_jaxpr/ppermute | solution.py:13
  397.2 18.4 %all-to-all-start = ((bf16[32,16,512]{2,0,1:T(8,128)(2,1)}), bf16[32,16,512]{2,0,1:T(8,128)(2,1)S(1)}, u32[]{:S(2)}, u32[]{:S(2)}) async-start(bf16[32,16,512]{2,0,1:T(8,128)(2,1)} %bitcast.109), calls=%async_computation | async-start | bytes 1048576 | tf_op jit(solution)/shard_map/while/body/eval_jaxpr/all_to_all | solution.py:99
  415.8 5.8 %collective-permute-start.1 = (bf16[32,512]{1,0:T(8,128)(2,1)S(1)}, bf16[32,512]{1,0:T(8,128)(2,1)S(1)}, u32[]{:S(2)}, u32[]{:S(2)}) collective-permute-start(bf16[32,512]{1,0:T(8,128)(2,1)S(1)} %fusion.38), channel_id=1, source_target_pairs={{16,0},{17,1},{18,2},{19,3},{20,4},{21,5},{22,6},{23,7},{24,8},{25... | collective-permute-start | bytes 98312 | tf_op jit(solution)/shard_map/while/body/eval_jaxpr/ppermute | solution.py:13
  428.4 18.4 %all-to-all-start = ((bf16[32,16,512]{2,0,1:T(8,128)(2,1)}), bf16[32,16,512]{2,0,1:T(8,128)(2,1)S(1)}, u32[]{:S(2)}, u32[]{:S(2)}) async-start(bf16[32,16,512]{2,0,1:T(8,128)(2,1)} %bitcast.109), calls=%async_computation | async-start | bytes 1048576 | tf_op jit(solution)/shard_map/while/body/eval_jaxpr/all_to_all | solution.py:99
  447.0 5.8 %collective-permute-start.1 = (bf16[32,512]{1,0:T(8,128)(2,1)S(1)}, bf16[32,512]{1,0:T(8,128)(2,1)S(1)}, u32[]{:S(2)}, u32[]{:S(2)}) collective-permute-start(bf16[32,512]{1,0:T(8,128)(2,1)S(1)} %fusion.38), channel_id=1, source_target_pairs={{16,0},{17,1},{18,2},{19,3},{20,4},{21,5},{22,6},{23,7},{24,8},{25... | collective-permute-start | bytes 98312 | tf_op jit(solution)/shard_map/while/body/eval_jaxpr/ppermute | solution.py:13
where the time goes:
time: 497 us; the launch traced here: 495 us
  blocking collectives  252 us (51%)
  waiting for transfers between devices  98.3 us (20%)
  matrix products  76.6 us (15%)
  starting transfers between devices  49.8 us (10%)
  other arithmetic  8.44 us (2%)
  local copies, waits for them, and re-layouts  5.69 us (1%)
    all_gather x5, blocking collectives, forward_tick(): shard_piece = lax.all_gather(layer_in, 'mp', axis=1, tiled=True)  97 us
    all_to_all x5, waiting for transfers between devices, backward_tick(): lax.all_to_all(partial_term.astype(jnp.bfloat16), 'mp', split_axis=1, con...  71.2 us
    psum x1, blocking collectives, power_step(): lax.psum(jnp.dot(weight, vector_bf, preferred_element_type=jnp.float32),...  63 us
    psum x1, blocking collectives, on_device(): lax.psum(jnp.sum(outer_sum * weight.astype(jnp.float32)), 'mp')  31.7 us
    psum x1, blocking collectives, on_device(): logits_all = lax.psum(partial_logits, 'mp')  30.4 us
    psum x1, blocking collectives, power_step(): norm_total = lax.psum(jnp.sum(right_part * right_part), 'mp')  30.1 us
    ppermute x10, starting transfers between devices, shifted(): return lax.ppermute(block, axis, route)  29.6 us
    dot_general x5, matrix products, backward_tick(): lax.dot_general(grad_pre, weight, (((1,), (1,)), ((), ())), preferred_ele...  29.6 us
  transfers between devices with their start and end apart: 15, of which 15 were waited for; matrix products, arithmetic and copies ran while one was open for 0% of the time, Pallas kernels for 0%

commit v1 on v0

--- a/solution.py
+++ b/solution.py
@@ -79,7 +79,11 @@
     _, inputs_all, pre_all, partial_logits, spectral, new_u = lax.fori_loop(
         0, tick_count, forward_tick, start_state
     )
-    logits_all = lax.psum(partial_logits, "mp")
+    logits_all = partial_logits
+    for hop in (1, 2, 4, 8):
+        logits_all = logits_all + lax.ppermute(
+            logits_all, "mp", [(dev, dev ^ hop) for dev in range(16)]
+        )
 
     def backward_tick(tick_now, state_all):
         incoming, grad_all = state_all

time: 497 us -> 478 us (0.962)
  blocking collectives: 252 us -> 222 us
  waiting for transfers between devices: 98.3 us -> 108 us
    psum x1 -> x0, blocking collectives: 30.4 us -> none  [on_device(): logits_all = lax.psum(partial_logits, 'mp')]
    ppermute x0 -> x4, waiting for transfers between devices: none -> 9.68 us  [on_device(): lax.ppermute(logits_all, 'mp', [(dev, dev ^ hop) for dev in range(16)])]
  transfers between devices with their start and end apart: 15 -> 19, of which waited for: 15 -> 19; matrix products, arithmetic and copies ran while one was open for 0% -> 1% of each run, Pallas kernels for 0% -> 0%
where the time goes in v1:
time: 478 us; the launch traced here: 476 us
  blocking collectives  222 us (46%)
  waiting for transfers between devices  108 us (23%)
  matrix products  76.6 us (16%)
  starting transfers between devices  51.6 us (11%)
  other arithmetic  8.44 us (2%)
  local copies, waits for them, and re-layouts  5.69 us (1%)
    all_gather x5, blocking collectives, forward_tick(): shard_piece = lax.all_gather(layer_in, 'mp', axis=1, tiled=True)  97 us
    all_to_all x5, waiting for transfers between devices, backward_tick(): lax.all_to_all(partial_term.astype(jnp.bfloat16), 'mp', split_axis=1, con...  71.2 us
    psum x1, blocking collectives, power_step(): lax.psum(jnp.dot(weight, vector_bf, preferred_element_type=jnp.float32),...  63 us
    psum x1, blocking collectives, on_device(): lax.psum(jnp.sum(outer_sum * weight.astype(jnp.float32)), 'mp')  31.7 us
    psum x1, blocking collectives, power_step(): norm_total = lax.psum(jnp.sum(right_part * right_part), 'mp')  30.1 us
    ppermute x10, starting transfers between devices, shifted(): return lax.ppermute(block, axis, route)  29.6 us
    dot_general x5, matrix products, backward_tick(): lax.dot_general(grad_pre, weight, (((1,), (1,)), ((), ())), preferred_ele...  29.6 us
    dot_general x5, matrix products, forward_tick(): jnp.dot(shard_piece, weight, preferred_element_type=jnp.float32)  28.3 us
  transfers between devices with their start and end apart: 19, of which 19 were waited for; matrix products, arithmetic and copies ran while one was open for 1% of the time, Pallas kernels for 0%

profile of v1, /device:TPU:0, one launch (start us, length us, event | category | flops | bytes accessed | tf_op | source)
XLA Modules:
  0.0 476.5 jit_solution(14155756928762305465)
XLA Ops:
  6.3 63.0 %psum.21 = f32[8192]{0:T(1024)S(1)} all-reduce(f32[8192]{0:T(1024)S(1)} %bitcast.113), channel_id=1, replica_groups=mesh['section'=2,'mp'=16] {'mp'}, use_global_device_ids=true, to_apply=%region_0.0 | all-reduce | flops 8192 | bytes 65536 | tf_op jit(solution)/shard_map/psum | solution.py:30
  75.8 30.1 %psum.22 = f32[]{:T(128)} all-reduce(f32[]{:T(128)} %multiply_reduce_fusion.2), channel_id=1, replica_groups=mesh['section'=2,'mp'=16] {'mp'}, use_global_device_ids=true, to_apply=%region_3.0 | all-reduce | flops 1 | bytes 8 | tf_op jit(solution)/shard_map/psum | solution.py:33
  107.4 158.8 %while.37 = (s32[]{:T(128)}, bf16[32,512]{1,0:T(8,128)(2,1)}, bf16[4,32,8192]{2,1,0:T(8,128)(2,1)S(1)}, f32[4,32,512]{2,1,0:T(8,128)S(1)}, f32[4,32]{1,0:T(4,128...) while((s32[]{:T(128)}, bf16[32,512]{1,0:T(8,128)(2,1)}, ...), condition=%wide.region_6.7_spmd, body=%wide.region_4.6_spmd.sunk | while | flops 268910592 | bytes 12782621 | solution.py:79
  108.2 18.7 %all_gather.9 = bf16[32,8192]{1,0:T(8,128)(2,1)S(1)} all-gather(bf16[32,512]{1,0:T(8,128)(2,1)S(1)} %bitcast_select_fusion.5), channel_id=1, replica_groups=mesh['section'=2,'mp'=16] {'mp'}, dimensions={1}, use_global_device_ids=true | all-gather | bytes 557056 | tf_op jit(solution)/shard_map/while/body/eval_jaxpr/all_gather | solution.py:56
  126.9 5.7 %multiply_reduce_fusion.4 = (f32[32]{0:T(128)S(1)}, bf16[32,512]{1,0:T(8,128)(2,1)}, f32[32,512]{1,0:T(8,128)S(1)}) fusion(f32[512]{0:T(512)S(1)} %get-tuple-element.704, bf16[32,512]{1,0:T(8,128)(2,1)S(1)} %bitcast_select_fusion.5, f32[]{:T(128)} %get-tuple-element.702, bf16[32,8192]{1,0:T(8,128)(2,1)S(1)} %all_gather.9, ...), kind=kOutput, calls=%fused_computation.5.clone.1 | convolution fusion | flops 268615648 | bytes 9046148 | tf_op jit(solution)/shard_map/while/body/eval_jaxpr/dot_general | solution.py:57
  138.6 20.4 %all_gather.9 = bf16[32,8192]{1,0:T(8,128)(2,1)S(1)} all-gather(bf16[32,512]{1,0:T(8,128)(2,1)S(1)} %bitcast_select_fusion.5), channel_id=1, replica_groups=mesh['section'=2,'mp'=16] {'mp'}, dimensions={1}, use_global_device_ids=true | all-gather | bytes 557056 | tf_op jit(solution)/shard_map/while/body/eval_jaxpr/all_gather | solution.py:56
  171.6 18.7 %all_gather.9 = bf16[32,8192]{1,0:T(8,128)(2,1)S(1)} all-gather(bf16[32,512]{1,0:T(8,128)(2,1)S(1)} %bitcast_select_fusion.5), channel_id=1, replica_groups=mesh['section'=2,'mp'=16] {'mp'}, dimensions={1}, use_global_device_ids=true | all-gather | bytes 557056 | tf_op jit(solution)/shard_map/while/body/eval_jaxpr/all_gather | solution.py:56
  190.3 5.7 %multiply_reduce_fusion.4 = (f32[32]{0:T(128)S(1)}, bf16[32,512]{1,0:T(8,128)(2,1)}, f32[32,512]{1,0:T(8,128)S(1)}) fusion(f32[512]{0:T(512)S(1)} %get-tuple-element.704, bf16[32,512]{1,0:T(8,128)(2,1)S(1)} %bitcast_select_fusion.5, f32[]{:T(128)} %get-tuple-element.702, bf16[32,8192]{1,0:T(8,128)(2,1)S(1)} %all_gather.9, ...), kind=kOutput, calls=%fused_computation.5.clone.1 | convolution fusion | flops 268615648 | bytes 9046148 | tf_op jit(solution)/shard_map/while/body/eval_jaxpr/dot_general | solution.py:57
  202.8 20.4 %all_gather.9 = bf16[32,8192]{1,0:T(8,128)(2,1)S(1)} all-gather(bf16[32,512]{1,0:T(8,128)(2,1)S(1)} %bitcast_select_fusion.5), channel_id=1, replica_groups=mesh['section'=2,'mp'=16] {'mp'}, dimensions={1}, use_global_device_ids=true | all-gather | bytes 557056 | tf_op jit(solution)/shard_map/while/body/eval_jaxpr/all_gather | solution.py:56
  235.8 18.7 %all_gather.9 = bf16[32,8192]{1,0:T(8,128)(2,1)S(1)} all-gather(bf16[32,512]{1,0:T(8,128)(2,1)S(1)} %bitcast_select_fusion.5), channel_id=1, replica_groups=mesh['section'=2,'mp'=16] {'mp'}, dimensions={1}, use_global_device_ids=true | all-gather | bytes 557056 | tf_op jit(solution)/shard_map/while/body/eval_jaxpr/all_gather | solution.py:56
  254.5 5.7 %multiply_reduce_fusion.4 = (f32[32]{0:T(128)S(1)}, bf16[32,512]{1,0:T(8,128)(2,1)}, f32[32,512]{1,0:T(8,128)S(1)}) fusion(f32[512]{0:T(512)S(1)} %get-tuple-element.704, bf16[32,512]{1,0:T(8,128)(2,1)S(1)} %bitcast_select_fusion.5, f32[]{:T(128)} %get-tuple-element.702, bf16[32,8192]{1,0:T(8,128)(2,1)S(1)} %all_gather.9, ...), kind=kOutput, calls=%fused_computation.5.clone.1 | convolution fusion | flops 268615648 | bytes 9046148 | tf_op jit(solution)/shard_map/while/body/eval_jaxpr/dot_general | solution.py:57
  279.1 155.4 %while.38 = (s32[]{:T(128)}, bf16[32,512]{1,0:T(8,128)(2,1)S(1)}, bf16[4,32,512]{2,1,0:T(8,128)(2,1)S(1)}, pred[]{:T(512)}, s32[]{:T(128)}, /*index=5*/f32[4,32]...) while((s32[]{:T(128)}, bf16[32,512]{1,0:T(8,128)(2,1)S(1)}, ...), condition=%wide.region_9.10_spmd, body=%wide.region_7.9_spmd.sunk | while | flops 269762784 | bytes 12787494 | solution.py:116
  279.1 5.9 %convolution_convert_fusion.2 = bf16[32,8192]{1,0:T(8,128)(2,1)S(1)} fusion(bf16[8192,512]{1,0:T(8,128)(2,1)} %get-tuple-element.748, f32[4,32,512]{2,1,0:T(8,128)S(1)} %get-tuple-element.747, s32[]{:T(128)S(6)} %min.21, bf16[32,512]{1,0:T(8,128)(2,1)S(1)} %get-tuple-element.725, f32[512]{0:T(512)S(1)} %get-tuple-element.746, f32[32]{0:T(128)S(1)} %fusion.37, ...), kind=kOutput, calls=%fused_computation.12.clone.1 | convolution fusion | flops 268910592 | bytes 9013765 | tf_op jit(solution)/shard_map/while/body/eval_jaxpr/dot_general | solution.py:100
  289.5 14.2 %all-to-all-done = bf16[32,16,512]{2,0,1:T(8,128)(2,1)S(1)} async-done(((bf16[32,16,512]{2,0,1:T(8,128)(2,1)}), bf16[32,16,512]{2,0,1:T(8,128)(2,1)S(1)}, u32[]{:S(2)}, u32[]{:S(2)}) %all-to-all-start) | async-done | bytes 524320 | tf_op jit(solution)/shard_map/while/body/eval_jaxpr/all_to_all | solution.py:103
  309.7 5.9 %convolution_convert_fusion.2 = bf16[32,8192]{1,0:T(8,128)(2,1)S(1)} fusion(bf16[8192,512]{1,0:T(8,128)(2,1)} %get-tuple-element.748, f32[4,32,512]{2,1,0:T(8,128)S(1)} %get-tuple-element.747, s32[]{:T(128)S(6)} %min.21, bf16[32,512]{1,0:T(8,128)(2,1)S(1)} %get-tuple-element.725, f32[512]{0:T(512)S(1)} %get-tuple-element.746, f32[32]{0:T(128)S(1)} %fusion.37, ...), kind=kOutput, calls=%fused_computation.12.clone.1 | convolution fusion | flops 268910592 | bytes 9013765 | tf_op jit(solution)/shard_map/while/body/eval_jaxpr/dot_general | solution.py:100
  320.6 14.2 %all-to-all-done = bf16[32,16,512]{2,0,1:T(8,128)(2,1)S(1)} async-done(((bf16[32,16,512]{2,0,1:T(8,128)(2,1)}), bf16[32,16,512]{2,0,1:T(8,128)(2,1)S(1)}, u32[]{:S(2)}, u32[]{:S(2)}) %all-to-all-start) | async-done | bytes 524320 | tf_op jit(solution)/shard_map/while/body/eval_jaxpr/all_to_all | solution.py:103
  340.9 5.9 %convolution_convert_fusion.2 = bf16[32,8192]{1,0:T(8,128)(2,1)S(1)} fusion(bf16[8192,512]{1,0:T(8,128)(2,1)} %get-tuple-element.748, f32[4,32,512]{2,1,0:T(8,128)S(1)} %get-tuple-element.747, s32[]{:T(128)S(6)} %min.21, bf16[32,512]{1,0:T(8,128)(2,1)S(1)} %get-tuple-element.725, f32[512]{0:T(512)S(1)} %get-tuple-element.746, f32[32]{0:T(128)S(1)} %fusion.37, ...), kind=kOutput, calls=%fused_computation.12.clone.1 | convolution fusion | flops 268910592 | bytes 9013765 | tf_op jit(solution)/shard_map/while/body/eval_jaxpr/dot_general | solution.py:100
  351.9 14.2 %all-to-all-done = bf16[32,16,512]{2,0,1:T(8,128)(2,1)S(1)} async-done(((bf16[32,16,512]{2,0,1:T(8,128)(2,1)}), bf16[32,16,512]{2,0,1:T(8,128)(2,1)S(1)}, u32[]{:S(2)}, u32[]{:S(2)}) %all-to-all-start) | async-done | bytes 524320 | tf_op jit(solution)/shard_map/while/body/eval_jaxpr/all_to_all | solution.py:103
  372.1 5.9 %convolution_convert_fusion.2 = bf16[32,8192]{1,0:T(8,128)(2,1)S(1)} fusion(bf16[8192,512]{1,0:T(8,128)(2,1)} %get-tuple-element.748, f32[4,32,512]{2,1,0:T(8,128)S(1)} %get-tuple-element.747, s32[]{:T(128)S(6)} %min.21, bf16[32,512]{1,0:T(8,128)(2,1)S(1)} %get-tuple-element.725, f32[512]{0:T(512)S(1)} %get-tuple-element.746, f32[32]{0:T(128)S(1)} %fusion.37, ...), kind=kOutput, calls=%fused_computation.12.clone.1 | convolution fusion | flops 268910592 | bytes 9013765 | tf_op jit(solution)/shard_map/while/body/eval_jaxpr/dot_general | solution.py:100
  383.1 14.2 %all-to-all-done = bf16[32,16,512]{2,0,1:T(8,128)(2,1)S(1)} async-done(((bf16[32,16,512]{2,0,1:T(8,128)(2,1)}), bf16[32,16,512]{2,0,1:T(8,128)(2,1)S(1)}, u32[]{:S(2)}, u32[]{:S(2)}) %all-to-all-start) | async-done | bytes 524320 | tf_op jit(solution)/shard_map/while/body/eval_jaxpr/all_to_all | solution.py:103
  403.3 5.9 %convolution_convert_fusion.2 = bf16[32,8192]{1,0:T(8,128)(2,1)S(1)} fusion(bf16[8192,512]{1,0:T(8,128)(2,1)} %get-tuple-element.748, f32[4,32,512]{2,1,0:T(8,128)S(1)} %get-tuple-element.747, s32[]{:T(128)S(6)} %min.21, bf16[32,512]{1,0:T(8,128)(2,1)S(1)} %get-tuple-element.725, f32[512]{0:T(512)S(1)} %get-tuple-element.746, f32[32]{0:T(128)S(1)} %fusion.37, ...), kind=kOutput, calls=%fused_computation.12.clone.1 | convolution fusion | flops 268910592 | bytes 9013765 | tf_op jit(solution)/shard_map/while/body/eval_jaxpr/dot_general | solution.py:100
  414.3 14.2 %all-to-all-done = bf16[32,16,512]{2,0,1:T(8,128)(2,1)S(1)} async-done(((bf16[32,16,512]{2,0,1:T(8,128)(2,1)}), bf16[32,16,512]{2,0,1:T(8,128)(2,1)S(1)}, u32[]{:S(2)}, u32[]{:S(2)}) %all-to-all-start) | async-done | bytes 524320 | tf_op jit(solution)/shard_map/while/body/eval_jaxpr/all_to_all | solution.py:103
  434.5 8.5 %fusion.13 = (f32[]{:T(128)}, bf16[1,8192,512]{2,1,0:T(8,128)(2,1)}) fusion(bf16[1,8192,512]{2,1,0:T(8,128)(2,1)} %bitcast.111, f32[]{:T(128)} %sqrt.3, bf16[4,32,8192]{2,1,0:T(8,128)(2,1)S(1)} %get-tuple-element.460, bf16[4,32,512]{2,1,0:T(8,128)(2,1)S(1)} %get-tuple-element.463), kind=kOutput, calls=%fused_computation.40 | convolution fusion | flops 1094713344 | bytes 19005448 | tf_op jit(solution)/shard_map/dot_general | solution.py:119
  443.0 31.7 %psum.23 = f32[]{:T(128)} all-reduce(f32[]{:T(128)} %get-tuple-element.513), channel_id=1, replica_groups=mesh['section'=2,'mp'=16] {'mp'}, use_global_device_ids=true, to_apply=%region_11.12 | all-reduce | flops 1 | bytes 8 | tf_op jit(solution)/shard_map/psum | solution.py:123
  (125 shorter events, 124.1 us)
Async XLA Ops:
  70.6 36.8 %copy-start = (f32[512]{0:T(512)S(1)}, f32[512]{0:T(512)}, u32[]{:S(2)}) copy-start(f32[512]{0:T(512)} %param.13) | copy-start | bytes 6148
  132.5 5.3 %collective-permute-start = (bf16[32,512]{1,0:T(8,128)(2,1)}, bf16[32,512]{1,0:T(8,128)(2,1)}, u32[]{:S(2)}, u32[]{:S(2)}) collective-permute-start(bf16[32,512]{1,0:T(8,128)(2,1)} %get-tuple-element.647), channel_id=1, source_target_pairs={{0,16},{1,17},{2,18},{3,19},{4,20},{5,21},{6,22},{7,23},{8,24},{9,... | collective-permute-start | bytes 98312 | tf_op jit(solution)/shard_map/while/body/eval_jaxpr/ppermute | solution.py:13
  164.7 6.1 %collective-permute-start = (bf16[32,512]{1,0:T(8,128)(2,1)}, bf16[32,512]{1,0:T(8,128)(2,1)}, u32[]{:S(2)}, u32[]{:S(2)}) collective-permute-start(bf16[32,512]{1,0:T(8,128)(2,1)} %get-tuple-element.647), channel_id=1, source_target_pairs={{0,16},{1,17},{2,18},{3,19},{4,20},{5,21},{6,22},{7,23},{8,24},{9,... | collective-permute-start | bytes 98312 | tf_op jit(solution)/shard_map/while/body/eval_jaxpr/ppermute | solution.py:13
  195.9 6.1 %collective-permute-start = (bf16[32,512]{1,0:T(8,128)(2,1)}, bf16[32,512]{1,0:T(8,128)(2,1)}, u32[]{:S(2)}, u32[]{:S(2)}) collective-permute-start(bf16[32,512]{1,0:T(8,128)(2,1)} %get-tuple-element.647), channel_id=1, source_target_pairs={{0,16},{1,17},{2,18},{3,19},{4,20},{5,21},{6,22},{7,23},{8,24},{9,... | collective-permute-start | bytes 98312 | tf_op jit(solution)/shard_map/while/body/eval_jaxpr/ppermute | solution.py:13
  228.9 6.1 %collective-permute-start = (bf16[32,512]{1,0:T(8,128)(2,1)}, bf16[32,512]{1,0:T(8,128)(2,1)}, u32[]{:S(2)}, u32[]{:S(2)}) collective-permute-start(bf16[32,512]{1,0:T(8,128)(2,1)} %get-tuple-element.647), channel_id=1, source_target_pairs={{0,16},{1,17},{2,18},{3,19},{4,20},{5,21},{6,22},{7,23},{8,24},{9,... | collective-permute-start | bytes 98312 | tf_op jit(solution)/shard_map/while/body/eval_jaxpr/ppermute | solution.py:13
  260.1 6.1 %collective-permute-start = (bf16[32,512]{1,0:T(8,128)(2,1)}, bf16[32,512]{1,0:T(8,128)(2,1)}, u32[]{:S(2)}, u32[]{:S(2)}) collective-permute-start(bf16[32,512]{1,0:T(8,128)(2,1)} %get-tuple-element.647), channel_id=1, source_target_pairs={{0,16},{1,17},{2,18},{3,19},{4,20},{5,21},{6,22},{7,23},{8,24},{9,... | collective-permute-start | bytes 98312 | tf_op jit(solution)/shard_map/while/body/eval_jaxpr/ppermute | solution.py:13
  266.2 1.2 collective-permute-start.2
  267.4 3.6 collective-permute-start.3
  271.0 3.6 collective-permute-start.4
  274.6 4.5 collective-permute-start.5
  285.9 17.8 %all-to-all-start = ((bf16[32,16,512]{2,0,1:T(8,128)(2,1)}), bf16[32,16,512]{2,0,1:T(8,128)(2,1)S(1)}, u32[]{:S(2)}, u32[]{:S(2)}) async-start(bf16[32,16,512]{2,0,1:T(8,128)(2,1)} %bitcast.109), calls=%async_computation | async-start | bytes 1048576 | tf_op jit(solution)/shard_map/while/body/eval_jaxpr/all_to_all | solution.py:103
  303.9 5.8 %collective-permute-start.1 = (bf16[32,512]{1,0:T(8,128)(2,1)S(1)}, bf16[32,512]{1,0:T(8,128)(2,1)S(1)}, u32[]{:S(2)}, u32[]{:S(2)}) collective-permute-start(bf16[32,512]{1,0:T(8,128)(2,1)S(1)} %fusion.38), channel_id=1, source_target_pairs={{16,0},{17,1},{18,2},{19,3},{20,4},{21,5},{22,6},{23,7},{24,8},{25... | collective-permute-start | bytes 98312 | tf_op jit(solution)/shard_map/while/body/eval_jaxpr/ppermute | solution.py:13
  316.5 18.4 %all-to-all-start = ((bf16[32,16,512]{2,0,1:T(8,128)(2,1)}), bf16[32,16,512]{2,0,1:T(8,128)(2,1)S(1)}, u32[]{:S(2)}, u32[]{:S(2)}) async-start(bf16[32,16,512]{2,0,1:T(8,128)(2,1)} %bitcast.109), calls=%async_computation | async-start | bytes 1048576 | tf_op jit(solution)/shard_map/while/body/eval_jaxpr/all_to_all | solution.py:103
  335.0 5.8 %collective-permute-start.1 = (bf16[32,512]{1,0:T(8,128)(2,1)S(1)}, bf16[32,512]{1,0:T(8,128)(2,1)S(1)}, u32[]{:S(2)}, u32[]{:S(2)}) collective-permute-start(bf16[32,512]{1,0:T(8,128)(2,1)S(1)} %fusion.38), channel_id=1, source_target_pairs={{16,0},{17,1},{18,2},{19,3},{20,4},{21,5},{22,6},{23,7},{24,8},{25... | collective-permute-start | bytes 98312 | tf_op jit(solution)/shard_map/while/body/eval_jaxpr/ppermute | solution.py:13
  347.7 18.4 %all-to-all-start = ((bf16[32,16,512]{2,0,1:T(8,128)(2,1)}), bf16[32,16,512]{2,0,1:T(8,128)(2,1)S(1)}, u32[]{:S(2)}, u32[]{:S(2)}) async-start(bf16[32,16,512]{2,0,1:T(8,128)(2,1)} %bitcast.109), calls=%async_computation | async-start | bytes 1048576 | tf_op jit(solution)/shard_map/while/body/eval_jaxpr/all_to_all | solution.py:103
  366.3 5.8 %collective-permute-start.1 = (bf16[32,512]{1,0:T(8,128)(2,1)S(1)}, bf16[32,512]{1,0:T(8,128)(2,1)S(1)}, u32[]{:S(2)}, u32[]{:S(2)}) collective-permute-start(bf16[32,512]{1,0:T(8,128)(2,1)S(1)} %fusion.38), channel_id=1, source_target_pairs={{16,0},{17,1},{18,2},{19,3},{20,4},{21,5},{22,6},{23,7},{24,8},{25... | collective-permute-start | bytes 98312 | tf_op jit(solution)/shard_map/while/body/eval_jaxpr/ppermute | solution.py:13
  378.9 18.4 %all-to-all-start = ((bf16[32,16,512]{2,0,1:T(8,128)(2,1)}), bf16[32,16,512]{2,0,1:T(8,128)(2,1)S(1)}, u32[]{:S(2)}, u32[]{:S(2)}) async-start(bf16[32,16,512]{2,0,1:T(8,128)(2,1)} %bitcast.109), calls=%async_computation | async-start | bytes 1048576 | tf_op jit(solution)/shard_map/while/body/eval_jaxpr/all_to_all | solution.py:103
  397.5 5.8 %collective-permute-start.1 = (bf16[32,512]{1,0:T(8,128)(2,1)S(1)}, bf16[32,512]{1,0:T(8,128)(2,1)S(1)}, u32[]{:S(2)}, u32[]{:S(2)}) collective-permute-start(bf16[32,512]{1,0:T(8,128)(2,1)S(1)} %fusion.38), channel_id=1, source_target_pairs={{16,0},{17,1},{18,2},{19,3},{20,4},{21,5},{22,6},{23,7},{24,8},{25... | collective-permute-start | bytes 98312 | tf_op jit(solution)/shard_map/while/body/eval_jaxpr/ppermute | solution.py:13
  410.1 18.4 %all-to-all-start = ((bf16[32,16,512]{2,0,1:T(8,128)(2,1)}), bf16[32,16,512]{2,0,1:T(8,128)(2,1)S(1)}, u32[]{:S(2)}, u32[]{:S(2)}) async-start(bf16[32,16,512]{2,0,1:T(8,128)(2,1)} %bitcast.109), calls=%async_computation | async-start | bytes 1048576 | tf_op jit(solution)/shard_map/while/body/eval_jaxpr/all_to_all | solution.py:103
  428.7 5.8 %collective-permute-start.1 = (bf16[32,512]{1,0:T(8,128)(2,1)S(1)}, bf16[32,512]{1,0:T(8,128)(2,1)S(1)}, u32[]{:S(2)}, u32[]{:S(2)}) collective-permute-start(bf16[32,512]{1,0:T(8,128)(2,1)S(1)} %fusion.38), channel_id=1, source_target_pairs={{16,0},{17,1},{18,2},{19,3},{20,4},{21,5},{22,6},{23,7},{24,8},{25... | collective-permute-start | bytes 98312 | tf_op jit(solution)/shard_map/while/body/eval_jaxpr/ppermute | solution.py:13
